TPU v7x, 32 devices: a whole 2x2x4 slice. The times are simulated.
32 devices in a mesh: region: 8 (over z, x), member: 4 (over y, core).
Axes of the slice: x: 2, y: 2, z: 4, core: 2. Of those that a mesh axis runs over, the one named last changes fastest.
Arguments:
- ensemble: bfloat16 [40, 131072], P('member', 'region'), may hold values from -6 to 6
- obs_value: float32 [1024, 128], P(('region', 'member')), may hold values from -8 to 8
- obs_var: float32 [1024, 128], P(('region', 'member')), may hold values from 0.1 to 1
- obs_point: int32 [1024, 128], P(('region', 'member')), may hold values from 0 to 16383
- owned_blocks: int32 [1024], P('region'), may hold values from 0 to 1023, each once
- infl_mean: float32 [1024], replicated, may hold values from 0.6 to 1.6
- infl_var: float32 [1024], replicated, may hold values from 0.0001 to 0.1
Outputs:
- inflated: bfloat16 [40, 131072], P('member', 'region')
- infl_post: float32 [1024], P(('region', 'member'))
Inputs may be any that keep to these rules, and one draw needn't show every extreme that they name: `obs_point`: index among the 16384 points of the observation's region; the observation belongs to the block of that point's slot. `owned_blocks`: every block id appears exactly once.
All inputs are finite; a program needn't handle non-finite values.
Results may differ from a plain program's by a relative error of at most 0.001.
Values sent between devices are 32-bit elements; how exact they have to be, the bound alone decides.
A program may use at most 64 MiB of HBM per device.

v0:
```python
import jax
import jax.numpy as jnp
from jax import lax
from jax.sharding import PartitionSpec as P


def posterior(sums, prior_mean, prior_var):
    innov_sum = sums[0]
    spread_sum = sums[1]
    error_sum = sums[2]
    spread_spread = sums[3]
    spread_error = sums[4]
    error_error = sums[5]
    weight_var = (
        2.0 * prior_mean * prior_mean * (1.0 + spread_spread)
        + 4.0 * prior_mean * spread_error
        + 2.0 * error_error
    )
    value = (prior_mean * weight_var + prior_var * spread_sum * (innov_sum - error_sum)) / (
        weight_var + prior_var * spread_sum * spread_sum
    )
    return jnp.maximum(value, 1.0)


def bin_slots(innovation, spread, errors, slot_of, slots):
    count = innovation.shape[0]
    width = min(count, 2048)
    while count % width != 0:
        width = width // 2
    blocks = count // width
    inno = innovation.reshape(blocks, width)
    sprd = spread.reshape(blocks, width)
    errs = errors.reshape(blocks, width)
    columns = jnp.stack([inno * inno, sprd, errs, sprd * sprd, sprd * errs, errs * errs], 1)
    labels = slot_of.reshape(blocks, width)
    slot_ids = jnp.arange(slots, dtype=jnp.int32)

    def one_block(carry, pair):
        block_cols, block_labels = pair
        onehot = (block_labels[:, None] == slot_ids[None, :]).astype(jnp.float32)
        return (
            carry
            + jnp.dot(
                block_cols,
                onehot,
                precision=lax.Precision.HIGHEST,
                preferred_element_type=jnp.float32,
            ),
            None,
        )

    total, unused = lax.scan(one_block, jnp.zeros((6, slots), jnp.float32), (columns, labels))
    return total


def body(ensemble, obs_value, obs_var, obs_point, owned_blocks, infl_mean, infl_var):
    members = ensemble.shape[0] * lax.axis_size("member")
    wide = ensemble.astype(jnp.float32)
    local_total = jnp.sum(wide, 0)
    local_square = jnp.sum(wide * wide, 0)
    own_points = obs_point.reshape(-1)
    point_total, point_square = lax.psum((local_total, local_square), "member")
    point_mean = point_total / members
    at_square = point_square[own_points]
    at_mean = point_mean[own_points]
    spread = (at_square - members * at_mean * at_mean) / (members - 1)
    innovation = obs_value.reshape(-1) - at_mean
    errors = obs_var.reshape(-1)
    slots = owned_blocks.shape[0]
    span = point_mean.shape[0] // slots
    slot_of = own_points // span
    slot_sums = bin_slots(innovation, spread, errors, slot_of, slots)
    num_blocks = infl_mean.shape[0]
    share = num_blocks // lax.axis_size(("region", "member"))
    first = lax.axis_index(("region", "member")) * share
    placed_sums = jnp.zeros((6, num_blocks), jnp.float32).at[:, owned_blocks].set(slot_sums)
    totals = lax.psum(placed_sums, ("region", "member"))
    lambda_all = posterior(totals, infl_mean, infl_var)
    lambda_mine = lax.dynamic_slice_in_dim(lambda_all, first, share)
    lambda_owned = lambda_all[owned_blocks]
    factor = jnp.sqrt(lambda_owned)[None, :, None]
    mean_slots = point_mean.reshape(1, slots, -1)
    shaped = wide.reshape(wide.shape[0], slots, -1)
    inflated = (
        (mean_slots + factor * (shaped - mean_slots)).astype(jnp.bfloat16).reshape(ensemble.shape)
    )
    return (inflated, lambda_mine)


def solution(mesh):
    placed = (
        P("member", "region"),
        P(("region", "member"), None),
        P(("region", "member"), None),
        P(("region", "member"), None),
        P("region"),
        P(),
        P(),
    )
    return jax.shard_map(
        body,
        mesh=mesh,
        in_specs=placed,
        out_specs=(P("member", "region"), P(("region", "member"))),
        check_vma=False,
    )
```

profile of v0, /device:TPU:0, one launch (start us, length us, event | category | flops | bytes accessed | tf_op | source)
XLA Modules:
  0.0 151.9 jit_solution(3200294530436090924)
XLA Ops:
  7.2 0.0 all-reduce.3.cloned.1.call-start
  7.2 2.2 %fusion.6 = (f32[16384]{0:T(1024)}, f32[16384]{0:T(1024)}) fusion(bf16[10,16384]{1,0:T(8,128)(2,1)} %param.9), kind=kLoop, calls=%fused_computation.15 | loop fusion | flops 622592 | bytes 458752 | tf_op jit(solution)/shard_map/reduce_sum | solution.py:60
  9.4 0.0 copy-start.3
  9.4 0.0 all-reduce.3.cloned.1.call-update
  9.4 0.7 copy-done.3
  10.2 0.0 copy-start.7
  10.2 0.6 copy-done.7
  10.9 34.6 %all-reduce.3.cloned.1.call-done = (f32[16384]{0:T(1024)}, f32[16384]{0:T(1024)}) async-done(((f32[16384]{0:T(1024)}, f32[16384]{0:T(1024)}), (f32[16384]{0:T(1024)}, f32[16384]{0:T(1024)})) %all-reduce.3.cloned.1.call-update) | async-done | bytes 131088 | tf_op jit(solution)/shard_map/psum | solution.py:62
  45.5 0.8 broadcast_multiply_fusion
  46.3 0.0 copy-start
  46.4 23.0 %gather_fusion = f32[4096]{0:T(1024)S(1)} fusion(f32[16384]{0:T(1024)S(1)} %broadcast_multiply_fusion, s32[4096]{0:T(1024)S(1)} %broadcast_clamp_fusion), kind=kCustom, calls=%fused_computation | custom fusion | bytes 49152 | tf_op jit(solution)/shard_map/gather | solution.py:65
  69.4 0.0 copy-done
  69.4 0.0 copy-start.2
  69.4 0.0 copy-start.4
  69.4 23.0 %gather_fusion.1 = f32[4096]{0:T(1024)S(1)} fusion(f32[16384]{0:T(1024)S(1)} %copy-done, s32[4096]{0:T(1024)S(1)} %broadcast_clamp_fusion), kind=kCustom, calls=%fused_computation.1 | custom fusion | bytes 49152 | tf_op jit(solution)/shard_map/gather | solution.py:64
  92.5 0.0 copy-done.2
  92.5 0.0 copy-done.4
  92.5 0.1 fusion.20
  92.6 0.2 stack.2
  92.7 1.2 while.11
  92.8 0.6 convolution_add_fusion.2
  93.4 0.6 convolution_add_fusion.2
  94.0 0.1 copy.10
  94.1 1.0 scatter_custom_fusion
  95.1 45.8 %psum.23 = f32[6,1024]{0,1:T(8,128)S(1)} all-reduce(f32[6,1024]{0,1:T(8,128)S(1)} %scatter_custom_fusion), channel_id=1, replica_groups=mesh['region'=8,'member'=4] {'region','member'}, use_global_device_ids=true, to_apply=%region_7.8 | all-reduce | flops 6144 | bytes 49152 | tf_op jit(solution)/shard_map/psum | solution.py:77
  140.9 0.0 copy-start.5
  141.0 0.0 copy-start.6
  141.0 1.4 slice_reduce_fusion.1
  142.4 0.0 copy-start.1
  142.4 0.0 copy-done.5
  142.4 0.0 copy-done.6
  142.5 1.0 gather_fusion.2
  143.5 0.1 broadcast_bitcast_fusion
  143.5 0.0 copy-done.1
  143.5 1.0 fusion.9
  144.5 0.6 dynamic_slice.11
  (12 shorter events, 0.2 us)
Async XLA Ops:
  7.2 38.3 %all-reduce.3.cloned.1.call-start = ((), (), s32[]{:S(2)}) async-start(), calls=%async_computation | async-start | bytes 262144 | tf_op jit(solution)/shard_map/psum | solution.py:62
  9.4 0.7 copy-start.3
  10.2 0.7 copy-start.7
  46.3 23.0 %copy-start = (f32[16384]{0:T(1024)S(1)}, f32[16384]{0:T(1024)}, u32[]{:S(2)}) copy-start(f32[16384]{0:T(1024)} %get-tuple-element.63) | copy-start | bytes 196612
  69.4 23.1 %copy-start.2 = (f32[32,128]{1,0:T(8,128)S(1)}, f32[32,128]{1,0:T(8,128)}, u32[]{:S(2)}) copy-start(f32[32,128]{1,0:T(8,128)} %param.11) | copy-start | bytes 49156
  69.4 23.1 %copy-start.4 = (f32[32,128]{1,0:T(8,128)S(1)}, f32[32,128]{1,0:T(8,128)}, u32[]{:S(2)}) copy-start(f32[32,128]{1,0:T(8,128)} %param.10) | copy-start | bytes 49156
  140.9 1.5 copy-start.5
  141.0 1.5 copy-start.6
  142.4 1.1 copy-start.1
Sparse Core Ops, SparseCore 0:
  10.9 34.5 all-reduce.2
where the time goes:
time: 152 us
  local copies, waits for them, and re-layouts  50.4 us (33%)
  blocking collectives  45.8 us (30%)
  waiting for transfers between devices  34.6 us (23%)
  between operations  14.3 us (9%)
  other arithmetic  5.59 us (4%)
    psum x1, blocking collectives, body(): totals = lax.psum(placed_sums, ('region', 'member'))  45.8 us
    psum x1, waiting for transfers between devices, body(): point_total, point_square = lax.psum((local_total, local_square), 'member')  34.6 us
    gather x1, local copies, waits for them, and re-layouts, body(): at_mean = point_mean[own_points]  23 us
    gather x1, local copies, waits for them, and re-layouts, body(): at_square = point_square[own_points]  23 us
  transfers between devices with their start and end apart: 1, of which 1 were waited for; matrix products, arithmetic and copies ran while one was open for 0% of the time, Pallas kernels for 0%

commit v1 on v0

--- a/solution.py
+++ b/solution.py
@@ -2,6 +2,7 @@
 import jax.numpy as jnp
 from jax import lax
 from jax.sharding import PartitionSpec as P
+from jax.lax import psum
 
 
 def posterior(sums, prior_mean, prior_var):
@@ -74,7 +75,7 @@
     share = num_blocks // lax.axis_size(("region", "member"))
     first = lax.axis_index(("region", "member")) * share
     placed_sums = jnp.zeros((6, num_blocks), jnp.float32).at[:, owned_blocks].set(slot_sums)
-    totals = lax.psum(placed_sums, ("region", "member"))
+    totals = psum(psum(placed_sums, "member"), axis_name="region")
     lambda_all = posterior(totals, infl_mean, infl_var)
     lambda_mine = lax.dynamic_slice_in_dim(lambda_all, first, share)
     lambda_owned = lambda_all[owned_blocks]

time: 152 us -> 166 us (1.092)
  blocking collectives: 45.8 us -> 59.4 us
    psum x1 -> x2, blocking collectives: 45.8 us -> 59.4 us  [body(): totals = psum(psum(placed_sums, 'member'), axis_name='region')]
where the time goes in v1:
time: 166 us; the launch traced here: 165 us
  blocking collectives  59.4 us (36%)
  local copies, waits for them, and re-layouts  50.4 us (30%)
  waiting for transfers between devices  34.6 us (21%)
  between operations  14.3 us (9%)
  other arithmetic  5.59 us (3%)
    psum x2, blocking collectives, body(): totals = psum(psum(placed_sums, 'member'), axis_name='region')  59.4 us
    psum x1, waiting for transfers between devices, body(): point_total, point_square = lax.psum((local_total, local_square), 'member')  34.6 us
    gather x1, local copies, waits for them, and re-layouts, body(): at_mean = point_mean[own_points]  23 us
    gather x1, local copies, waits for them, and re-layouts, body(): at_square = point_square[own_points]  23 us
  transfers between devices with their start and end apart: 1, of which 1 were waited for; matrix products, arithmetic and copies ran while one was open for 0% of the time, Pallas kernels for 0%

profile of v1, /device:TPU:0, one launch (start us, length us, event | category | flops | bytes accessed | tf_op | source)
XLA Modules:
  0.0 165.5 jit_solution(12511674251205361608)
XLA Ops:
  7.2 0.0 all-reduce.3.cloned.1.call-start
  7.2 2.2 %fusion.6 = (f32[16384]{0:T(1024)}, f32[16384]{0:T(1024)}) fusion(bf16[10,16384]{1,0:T(8,128)(2,1)} %param.9), kind=kLoop, calls=%fused_computation.15 | loop fusion | flops 622592 | bytes 458752 | tf_op jit(solution)/shard_map/reduce_sum | solution.py:61
  9.4 0.0 copy-start.3
  9.4 0.0 all-reduce.3.cloned.1.call-update
  9.4 0.7 copy-done.3
  10.2 0.0 copy-start.7
  10.2 0.6 copy-done.7
  10.9 34.6 %all-reduce.3.cloned.1.call-done = (f32[16384]{0:T(1024)}, f32[16384]{0:T(1024)}) async-done(((f32[16384]{0:T(1024)}, f32[16384]{0:T(1024)}), (f32[16384]{0:T(1024)}, f32[16384]{0:T(1024)})) %all-reduce.3.cloned.1.call-update) | async-done | bytes 131088 | tf_op jit(solution)/shard_map/psum | solution.py:63
  45.5 0.8 broadcast_multiply_fusion
  46.3 0.0 copy-start
  46.4 23.0 %gather_fusion = f32[4096]{0:T(1024)S(1)} fusion(f32[16384]{0:T(1024)S(1)} %broadcast_multiply_fusion, s32[4096]{0:T(1024)S(1)} %broadcast_clamp_fusion), kind=kCustom, calls=%fused_computation | custom fusion | bytes 49152 | tf_op jit(solution)/shard_map/gather | solution.py:66
  69.4 0.0 copy-done
  69.4 0.0 copy-start.2
  69.4 0.0 copy-start.4
  69.4 23.0 %gather_fusion.1 = f32[4096]{0:T(1024)S(1)} fusion(f32[16384]{0:T(1024)S(1)} %copy-done, s32[4096]{0:T(1024)S(1)} %broadcast_clamp_fusion), kind=kCustom, calls=%fused_computation.1 | custom fusion | bytes 49152 | tf_op jit(solution)/shard_map/gather | solution.py:65
  92.5 0.0 copy-done.2
  92.5 0.0 copy-done.4
  92.5 0.1 fusion.20
  92.6 0.2 stack.2
  92.7 1.2 while.11
  92.8 0.6 convolution_add_fusion.2
  93.4 0.6 convolution_add_fusion.2
  94.0 0.1 copy.10
  94.1 1.0 scatter_custom_fusion
  95.1 16.0 %psum.30 = f32[6,1024]{0,1:T(8,128)S(1)} all-reduce(f32[6,1024]{0,1:T(8,128)S(1)} %scatter_custom_fusion), channel_id=1, replica_groups=mesh['region'=8,'member'=4] {'member'}, use_global_device_ids=true, to_apply=%region_7.8 | all-reduce | flops 6144 | bytes 49152 | tf_op jit(solution)/shard_map/psum | solution.py:78
  111.2 43.3 %psum.31 = f32[6,1024]{0,1:T(8,128)S(1)} all-reduce(f32[6,1024]{0,1:T(8,128)S(1)} %psum.30), channel_id=1, replica_groups=mesh['region'=8,'member'=4] {'region'}, use_global_device_ids=true, to_apply=%region_8.9 | all-reduce | flops 6144 | bytes 49152 | tf_op jit(solution)/shard_map/psum | solution.py:78
  154.5 0.0 copy-start.5
  154.5 0.0 copy-start.6
  154.5 1.4 slice_reduce_fusion.1
  156.0 0.0 copy-start.1
  156.0 0.0 copy-done.5
  156.0 0.0 copy-done.6
  156.0 1.0 gather_fusion.2
  157.0 0.1 broadcast_bitcast_fusion
  157.1 0.0 copy-done.1
  157.1 1.0 fusion.9
  158.1 0.6 dynamic_slice.11
  (12 shorter events, 0.2 us)
Async XLA Ops:
  7.2 38.3 %all-reduce.3.cloned.1.call-start = ((), (), s32[]{:S(2)}) async-start(), calls=%async_computation | async-start | bytes 262144 | tf_op jit(solution)/shard_map/psum | solution.py:63
  9.4 0.7 copy-start.3
  10.2 0.7 copy-start.7
  46.3 23.0 %copy-start = (f32[16384]{0:T(1024)S(1)}, f32[16384]{0:T(1024)}, u32[]{:S(2)}) copy-start(f32[16384]{0:T(1024)} %get-tuple-element.63) | copy-start | bytes 196612
  69.4 23.1 %copy-start.2 = (f32[32,128]{1,0:T(8,128)S(1)}, f32[32,128]{1,0:T(8,128)}, u32[]{:S(2)}) copy-start(f32[32,128]{1,0:T(8,128)} %param.11) | copy-start | bytes 49156
  69.4 23.1 %copy-start.4 = (f32[32,128]{1,0:T(8,128)S(1)}, f32[32,128]{1,0:T(8,128)}, u32[]{:S(2)}) copy-start(f32[32,128]{1,0:T(8,128)} %param.10) | copy-start | bytes 49156
  154.5 1.5 copy-start.5
  154.5 1.5 copy-start.6
  156.0 1.1 copy-start.1
Sparse Core Ops, SparseCore 0:
  10.9 34.5 all-reduce.2
